TPU v7x, 32 devices: a whole 2x2x4 slice. The times are simulated.
32 devices in a mesh: genes: 32 (over z, y, x, core).
Axes of the slice: x: 2, y: 2, z: 4, core: 2. Of those that a mesh axis runs over, the one named last changes fastest.
Arguments:
- expression: bfloat16 [32768, 1024], P('genes'), may hold values from -10 to 20
- labels: int32 [32768], P('genes'), may hold values from 0 to 399
Outputs:
- membership: float32 [32768, 400], P('genes')
- eigengenes: bfloat16 [400, 1024], replicated
All inputs are finite; a program needn't handle non-finite values.
Results may differ from a plain program's by a relative error of at most 0.0012.
The roundings to bfloat16 on the way count: a program that leaves them out, or rounds other values in their place, can miss the bound.
Values may be sent and summed in bfloat16 or wider, within the bound.
No kernel may reach another device: no remote copies, remote signals or barrier semaphores. Data moves between devices by JAX's collectives and lax.ppermute only.
A program may use at most 64 MiB of HBM per device.

v0:
```python
import jax
import jax.numpy as jnp
from jax import lax
from jax.sharding import PartitionSpec as P

SAMPLES = 1024
MODULES = 400
ITERS = 2
epsilon = 1e-05
sharpness = 30.0


def standardize(expression):
    values = expression.astype(jnp.float32)
    centre = jnp.mean(values, axis=1, keepdims=True)
    shifted = values - centre
    spread = jnp.mean(shifted * shifted, axis=1, keepdims=True)
    return (shifted * lax.rsqrt(spread + epsilon)).astype(jnp.bfloat16)


def shards(expression, labels):
    standard = standardize(expression)
    module_ids = jnp.arange(MODULES, dtype=jnp.int32)
    weights = (labels[:, None] == module_ids[None, :]).astype(jnp.bfloat16)
    shares = None
    eigengenes = None
    for iteration in range(ITERS):
        partial_value = lax.dot_general(
            weights, standard, (((0,), (0,)), ((), ())), preferred_element_type=jnp.float32
        )
        module_sums = lax.psum(partial_value, "genes")
        scale = lax.rsqrt(jnp.mean(module_sums * module_sums, axis=1, keepdims=True) + epsilon)
        eigengenes = (module_sums * scale).astype(jnp.bfloat16)
        correlation = (
            lax.dot_general(
                standard, eigengenes, (((1,), (1,)), ((), ())), preferred_element_type=jnp.float32
            )
            / SAMPLES
        )
        raised = jnp.exp(sharpness * correlation)
        shares = raised / jnp.sum(raised, axis=1, keepdims=True)
        weights = shares.astype(jnp.bfloat16)
    return (MODULES * shares, eigengenes)


def solution(mesh):
    placed = (P("genes", None), P("genes"))
    return jax.shard_map(
        shards, mesh=mesh, in_specs=placed, out_specs=(P("genes", None), P()), check_vma=False
    )
```

profile of v0, /device:TPU:0, one launch (start us, length us, event | category | flops | bytes accessed | tf_op | source)
XLA Modules:
  0.0 299.7 jit_solution(1048506449199865023)
XLA Ops:
  7.2 0.0 copy-start
  7.2 0.0 all-reduce.3.cloned.1.call-start
  7.2 2.1 convert_reduce_fusion
  9.3 0.1 copy-done
  9.4 0.7 fusion.2
  10.1 0.0 copy-start.5
  10.1 0.5 fusion.3
  10.7 1.3 copy-done.2
  12.0 0.0 copy-done.5
  12.0 2.4 fusion.4
  14.4 0.0 all-reduce.3.cloned.1.call-update
  14.4 0.0 all-reduce.5.cloned.1.call-start
  14.5 135.1 %all-reduce.3.cloned.1.call-done = f32[400,1024]{1,0:T(8,128)} async-done(((f32[400,1024]{1,0:T(8,128)}), f32[400,1024]{1,0:T(8,128)}) %all-reduce.3.cloned.1.call-update) | async-done | bytes 1638416 | tf_op jit(solution)/shard_map/psum | solution.py:31
  149.6 1.6 multiply_reduce_fusion.1
  151.2 2.5 fusion.9
  153.7 2.2 fusion.6
  155.9 0.0 all-reduce.5.cloned.1.call-update
  155.9 132.3 %all-reduce.5.cloned.1.call-done = f32[400,1024]{1,0:T(8,128)} async-done(((f32[400,1024]{1,0:T(8,128)}), f32[400,1024]{1,0:T(8,128)}) %all-reduce.5.cloned.1.call-update) | async-done | bytes 1638416 | tf_op jit(solution)/shard_map/psum | solution.py:31
  288.3 1.7 multiply_reduce_fusion
  290.0 0.2 copy-done.1
  290.2 0.1 multiply_convert_fusion
  290.4 0.0 copy-start.4
  290.4 1.1 fusion.10
  291.5 1.4 divide_multiply_fusion
  (9 shorter events, 0.0 us)
Async XLA Ops:
  7.2 2.2 copy-start
  7.2 142.4 %all-reduce.3.cloned.1.call-start = ((), (), s32[]{:S(2)}) async-start(), calls=%async_computation | async-start | bytes 3276800 | tf_op jit(solution)/shard_map/psum | solution.py:31
  10.1 1.9 copy-start.5
  10.7 1.4 copy-start.2
  14.4 136.8 %copy-start.3 = (bf16[1024,1024]{1,0:T(8,128)(2,1)S(1)}, bf16[1024,1024]{1,0:T(8,128)(2,1)}, u32[]{:S(2)}) copy-start(bf16[1024,1024]{1,0:T(8,128)(2,1)} %copy-done.2) | copy-start | bytes 6291460
  14.4 273.8 %all-reduce.5.cloned.1.call-start = ((), (), s32[]{:S(2)}) async-start(), calls=%async_computation.1 | async-start | bytes 3276800 | tf_op jit(solution)/shard_map/psum | solution.py:31
  288.3 1.9 copy-start.1
  290.4 1.1 copy-start.4
Sparse Core Ops, SparseCore 0:
  14.6 134.9 all-reduce.2
  156.1 132.1 all-reduce.4
where the time goes:
time: 300 us
  waiting for transfers between devices  267 us (89%)
  between operations  14.1 us (5%)
  other arithmetic  8.28 us (3%)
  matrix products  8.17 us (3%)
    psum x2, waiting for transfers between devices, shards(): module_sums = lax.psum(partial_value, 'genes')  267 us
  transfers between devices with their start and end apart: 2, of which 2 were waited for; matrix products, arithmetic and copies ran while one was open for 0% of the time, Pallas kernels for 0%

commit v1 on v0

--- a/solution.py
+++ b/solution.py
@@ -28,7 +28,11 @@
         partial_value = lax.dot_general(
             weights, standard, (((0,), (0,)), ((), ())), preferred_element_type=jnp.float32
         )
-        module_sums = lax.psum(partial_value, "genes")
+        module_sums = partial_value
+        for hop in (1, 2, 4, 8, 16):
+            module_sums = module_sums + lax.ppermute(
+                module_sums, "genes", [(dev, dev ^ hop) for dev in range(32)]
+            )
         scale = lax.rsqrt(jnp.mean(module_sums * module_sums, axis=1, keepdims=True) + epsilon)
         eigengenes = (module_sums * scale).astype(jnp.bfloat16)
         correlation = (

time: 300 us -> 388 us (1.29)
  waiting for transfers between devices: 267 us -> 361 us
  between operations: 14.1 us -> 0.8 us
  starting transfers between devices: 0.08 us -> 13.2 us
    ppermute x0 -> x10, waiting for transfers between devices: none -> 361 us  [shards(): lax.ppermute(module_sums, 'genes', [(dev, dev ^ hop) for dev in range(32)])]
    psum x2 -> x0, waiting for transfers between devices: 267 us -> none  [shards(): module_sums = lax.psum(partial_value, 'genes')]
    ppermute x0 -> x10, starting transfers between devices: none -> 13.2 us  [shards(): lax.ppermute(module_sums, 'genes', [(dev, dev ^ hop) for dev in range(32)])]
  transfers between devices with their start and end apart: 2 -> 10, of which waited for: 2 -> 10; matrix products, arithmetic and copies ran while one was open for 0% -> 0% of each run, Pallas kernels for 0% -> 0%
where the time goes in v1:
time: 388 us
  waiting for transfers between devices  361 us (93%)
  starting transfers between devices  13.2 us (3%)
  other arithmetic  8.45 us (2%)
  matrix products  4.49 us (1%)
    ppermute x10, waiting for transfers between devices, shards(): lax.ppermute(module_sums, 'genes', [(dev, dev ^ hop) for dev in range(32)])  361 us
    ppermute x10, starting transfers between devices, shards(): lax.ppermute(module_sums, 'genes', [(dev, dev ^ hop) for dev in range(32)])  13.2 us
  transfers between devices with their start and end apart: 10, of which 10 were waited for; matrix products, arithmetic and copies ran while one was open for 0% of the time, Pallas kernels for 0%

profile of v1, /device:TPU:0, one launch (start us, length us, event | category | flops | bytes accessed | tf_op | source)
XLA Modules:
  0.0 388.2 jit_solution(666301808717512389)
XLA Ops:
  0.6 2.1 convert_reduce_fusion
  2.9 0.7 fusion.2
  4.3 1.2 fusion.4
  6.0 3.1 collective-permute-done
  9.6 2.9 collective-permute-start.1
  12.5 36.1 %collective-permute-done.1 = f32[400,1024]{1,0:T(8,128)S(1)} collective-permute-done((f32[400,1024]{1,0:T(8,128)S(1)}, f32[400,1024]{1,0:T(8,128)S(1)}, u32[]{:S(2)}, u32[]{:S(2)}) %collective-permute-start.1) | collective-permute-done | bytes 1638432 | tf_op jit(solution)/shard_map/ppermute | solution.py:33
  48.9 1.8 collective-permute-start.2
  50.8 35.5 %collective-permute-done.2 = f32[400,1024]{1,0:T(8,128)S(1)} collective-permute-done((f32[400,1024]{1,0:T(8,128)S(1)}, f32[400,1024]{1,0:T(8,128)S(1)}, u32[]{:S(2)}, u32[]{:S(2)}) %collective-permute-start.2) | collective-permute-done | bytes 1638432 | tf_op jit(solution)/shard_map/ppermute | solution.py:33
  86.7 1.6 collective-permute-start.3
  88.3 34.9 %collective-permute-done.3 = f32[400,1024]{1,0:T(8,128)S(1)} collective-permute-done((f32[400,1024]{1,0:T(8,128)S(1)}, f32[400,1024]{1,0:T(8,128)S(1)}, u32[]{:S(2)}, u32[]{:S(2)}) %collective-permute-start.3) | collective-permute-done | bytes 1638432 | tf_op jit(solution)/shard_map/ppermute | solution.py:33
  123.5 2.3 collective-permute-start.4
  125.9 69.3 %collective-permute-done.4 = f32[400,1024]{1,0:T(8,128)S(1)} collective-permute-done((f32[400,1024]{1,0:T(8,128)S(1)}, f32[400,1024]{1,0:T(8,128)S(1)}, u32[]{:S(2)}, u32[]{:S(2)}) %collective-permute-start.4) | collective-permute-done | bytes 1638432 | tf_op jit(solution)/shard_map/ppermute | solution.py:33
  195.4 1.1 fusion.9
  196.5 1.0 fusion.6
  197.7 3.5 collective-permute-done.5
  201.5 1.0 collective-permute-start.6
  202.5 36.9 %collective-permute-done.6 = f32[400,1024]{1,0:T(8,128)S(1)} collective-permute-done((f32[400,1024]{1,0:T(8,128)S(1)}, f32[400,1024]{1,0:T(8,128)S(1)}, u32[]{:S(2)}, u32[]{:S(2)}) %collective-permute-start.6) | collective-permute-done | bytes 1638432 | tf_op jit(solution)/shard_map/ppermute | solution.py:33
  239.8 1.0 collective-permute-start.7
  240.8 36.1 %collective-permute-done.7 = f32[400,1024]{1,0:T(8,128)S(1)} collective-permute-done((f32[400,1024]{1,0:T(8,128)S(1)}, f32[400,1024]{1,0:T(8,128)S(1)}, u32[]{:S(2)}, u32[]{:S(2)}) %collective-permute-start.7) | collective-permute-done | bytes 1638432 | tf_op jit(solution)/shard_map/ppermute | solution.py:33
  277.4 36.0 %collective-permute-done.8 = f32[400,1024]{1,0:T(8,128)S(1)} collective-permute-done((f32[400,1024]{1,0:T(8,128)S(1)}, f32[400,1024]{1,0:T(8,128)S(1)}, u32[]{:S(2)}, u32[]{:S(2)}) %collective-permute-start.8) | collective-permute-done | bytes 1638432 | tf_op jit(solution)/shard_map/ppermute | solution.py:33
  313.8 1.8 collective-permute-start.9
  315.6 69.6 %collective-permute-done.9 = f32[400,1024]{1,0:T(8,128)S(1)} collective-permute-done((f32[400,1024]{1,0:T(8,128)S(1)}, f32[400,1024]{1,0:T(8,128)S(1)}, u32[]{:S(2)}, u32[]{:S(2)}) %collective-permute-start.9) | collective-permute-done | bytes 1638432 | tf_op jit(solution)/shard_map/ppermute | solution.py:33
  385.6 1.1 fusion.10
  386.8 1.4 divide_multiply_fusion
  (25 shorter events, 5.3 us)
Async XLA Ops:
  0.6 2.2 copy-start
  3.6 0.7 copy-start.2
  5.5 3.7 collective-permute-start
  9.6 39.0 %collective-permute-start.1 = (f32[400,1024]{1,0:T(8,128)S(1)}, f32[400,1024]{1,0:T(8,128)S(1)}, u32[]{:S(2)}, u32[]{:S(2)}) collective-permute-start(f32[400,1024]{1,0:T(8,128)S(1)} %add.59), channel_id=1, source_target_pairs={{0,2},{1,3},{2,0},{3,1},{4,6},{5,7},{6,4},{7,5},{8,10},{9,11},{10,... | collective-permute-start | bytes 4915208 | tf_op jit(solution)/shard_map/ppermute | solution.py:33
  48.9 37.3 %collective-permute-start.2 = (f32[400,1024]{1,0:T(8,128)S(1)}, f32[400,1024]{1,0:T(8,128)S(1)}, u32[]{:S(2)}, u32[]{:S(2)}) collective-permute-start(f32[400,1024]{1,0:T(8,128)S(1)} %add.60), channel_id=1, source_target_pairs={{0,4},{1,5},{2,6},{3,7},{4,0},{5,1},{6,2},{7,3},{8,12},{9,13},{10,... | collective-permute-start | bytes 4915208 | tf_op jit(solution)/shard_map/ppermute | solution.py:33
  86.7 36.5 %collective-permute-start.3 = (f32[400,1024]{1,0:T(8,128)S(1)}, f32[400,1024]{1,0:T(8,128)S(1)}, u32[]{:S(2)}, u32[]{:S(2)}) collective-permute-start(f32[400,1024]{1,0:T(8,128)S(1)} %add.61), channel_id=1, source_target_pairs={{0,8},{1,9},{2,10},{3,11},{4,12},{5,13},{6,14},{7,15},{8,0},{9,1},... | collective-permute-start | bytes 4915208 | tf_op jit(solution)/shard_map/ppermute | solution.py:33
  123.5 71.6 %collective-permute-start.4 = (f32[400,1024]{1,0:T(8,128)S(1)}, f32[400,1024]{1,0:T(8,128)S(1)}, u32[]{:S(2)}, u32[]{:S(2)}) collective-permute-start(f32[400,1024]{1,0:T(8,128)S(1)} %add.62), channel_id=1, source_target_pairs={{0,16},{1,17},{2,18},{3,19},{4,20},{5,21},{6,22},{7,23},{8,24},{9,... | collective-permute-start | bytes 4915208 | tf_op jit(solution)/shard_map/ppermute | solution.py:33
  197.6 3.6 collective-permute-start.5
  201.5 37.9 %collective-permute-start.6 = (f32[400,1024]{1,0:T(8,128)S(1)}, f32[400,1024]{1,0:T(8,128)S(1)}, u32[]{:S(2)}, u32[]{:S(2)}) collective-permute-start(f32[400,1024]{1,0:T(8,128)S(1)} %add.65), channel_id=1, source_target_pairs={{0,2},{1,3},{2,0},{3,1},{4,6},{5,7},{6,4},{7,5},{8,10},{9,11},{10,... | collective-permute-start | bytes 4915208 | tf_op jit(solution)/shard_map/ppermute | solution.py:33
  239.8 37.1 %collective-permute-start.7 = (f32[400,1024]{1,0:T(8,128)S(1)}, f32[400,1024]{1,0:T(8,128)S(1)}, u32[]{:S(2)}, u32[]{:S(2)}) collective-permute-start(f32[400,1024]{1,0:T(8,128)S(1)} %add.66), channel_id=1, source_target_pairs={{0,4},{1,5},{2,6},{3,7},{4,0},{5,1},{6,2},{7,3},{8,12},{9,13},{10,... | collective-permute-start | bytes 4915208 | tf_op jit(solution)/shard_map/ppermute | solution.py:33
  277.3 36.2 %collective-permute-start.8 = (f32[400,1024]{1,0:T(8,128)S(1)}, f32[400,1024]{1,0:T(8,128)S(1)}, u32[]{:S(2)}, u32[]{:S(2)}) collective-permute-start(f32[400,1024]{1,0:T(8,128)S(1)} %add.67), channel_id=1, source_target_pairs={{0,8},{1,9},{2,10},{3,11},{4,12},{5,13},{6,14},{7,15},{8,0},{9,1},... | collective-permute-start | bytes 4915208 | tf_op jit(solution)/shard_map/ppermute | solution.py:33
  313.8 71.3 %collective-permute-start.9 = (f32[400,1024]{1,0:T(8,128)S(1)}, f32[400,1024]{1,0:T(8,128)S(1)}, u32[]{:S(2)}, u32[]{:S(2)}) collective-permute-start(f32[400,1024]{1,0:T(8,128)S(1)} %add.68), channel_id=1, source_target_pairs={{0,16},{1,17},{2,18},{3,19},{4,20},{5,21},{6,22},{7,23},{8,24},{9,... | collective-permute-start | bytes 4915208 | tf_op jit(solution)/shard_map/ppermute | solution.py:33
  385.6 1.1 copy-start.1
